TPU v7x, 512 devices: a whole 4x8x8 slice. The times are simulated.
512 devices in a mesh: replica: 16 (over z, core), mp: 16 (over y, x_hi), refresh: 2 (over x_lo).
Axes of the slice: x: 4 (x_hi: 2, x_lo: 2; x = x_hi * 2 + x_lo), y: 8, z: 8, core: 2. Of those that a mesh axis runs over, the one named last changes fastest.
Arguments:
- grad_partial: bfloat16 [16, 2, 512, 8192], P('replica', 'refresh', 'mp'), may hold values from -63 to 63
- left_stats: float32 [2, 512, 8192], P('refresh', 'replica', 'mp'), may hold values from -4608 to 5120, as said below
- right_stats: float32 [2, 512, 8192], P('refresh', 'replica', 'mp'), may hold values from -4608 to 5120, as said below
- left_roots: float32 [2, 512, 8192], P('refresh', 'replica', 'mp'), may hold values from -1 to 1, as said below
- right_roots: float32 [2, 512, 8192], P('refresh', 'replica', 'mp'), may hold values from -1 to 1, as said below
- newton_counts: int32 [2, 16], replicated, may hold values from 1 to 4
- owner: int32 [2, 16], replicated, may hold values from 0 to 15, each once within a row
Outputs:
- update: float32 [2, 512, 8192], P('refresh', 'mp')
- new_left_stats: float32 [2, 512, 8192], P('refresh', 'replica', 'mp')
- new_right_stats: float32 [2, 512, 8192], P('refresh', 'replica', 'mp')
- new_left_roots: float32 [2, 512, 8192], P('refresh', 'replica', 'mp')
- new_right_roots: float32 [2, 512, 8192], P('refresh', 'replica', 'mp')
Inputs may be any that keep to these rules, and one draw needn't show every extreme that they name: Each row of owner names every owner index once. `left_stats`: every 512 x 512 block is symmetric positive definite. `right_stats`: every 512 x 512 block is symmetric positive definite. `left_roots`: every 512 x 512 block is symmetric. `right_roots`: every 512 x 512 block is symmetric.
All inputs are finite; a program needn't handle non-finite values.
Results may differ from a plain program's by a relative error of at most 0.0003.
Values may be sent and summed in bfloat16 or wider, within the bound.
No kernel may reach another device: no remote copies, remote signals or barrier semaphores. Data moves between devices by JAX's collectives and lax.ppermute only.
A program may use at most 64 MiB of HBM per device.

v0:
```python
import functools
import jax
import jax.numpy as jnp
from jax import lax
from jax.sharding import Mesh
from jax.sharding import PartitionSpec as P

MP = ("mp_0", "mp_1")
REPLICA = ("replica_0", "replica_1")
REPLICA_MP_REFRESH = ("replica_0", "replica_1", "mp_0", "mp_1", "refresh")
decay = 0.9
graft_eps = 1e-06


def split_up(shard, dim, count):
    before, after = (shard.shape[:dim], shard.shape[dim + 1 :])
    return jnp.moveaxis(shard.reshape(*before, count, -1, *after), dim, 0)


def summed_on_arrival(shard, axis, dim):
    tiles = split_up(shard, dim, lax.axis_size(axis))
    arrived = lax.all_to_all(tiles, axis, split_axis=0, concat_axis=0, tiled=True)
    return arrived.sum(axis=0)


def by_axis(shard, axes):
    return functools.reduce(lax.psum, axes, shard)


def side_by_side(arrays, axis, dim, along):
    widths = [a.shape[along] for a in arrays]
    both = jnp.concatenate(arrays, axis=along)
    filled = lax.all_gather(both, axis, axis=dim, tiled=True)
    return tuple(jnp.split(filled, [sum(widths[:k]) for k in range(1, len(widths))], axis=along))


def swapped(shard, axis, stride):
    return lax.ppermute(shard, axis, [(i, i ^ 1 << stride) for i in range(lax.axis_size(axis))])


def sent_to_all(shard, axis):
    count = lax.axis_size(axis)
    return lax.all_to_all(
        jnp.broadcast_to(shard[None], (count, *shard.shape)), axis, 0, 0, tiled=True
    )


def laid_out(tiles, dim):
    lengths = list(tiles.shape[1:])
    lengths[dim] *= tiles.shape[0]
    return jnp.moveaxis(tiles, 0, dim).reshape(lengths)


def gather_directly(shard, axis, dim):
    tiles = sent_to_all(shard, axis)
    return laid_out(tiles, dim)


def product(left, right):
    return jnp.dot(left, right, precision=lax.Precision.HIGHEST, preferred_element_type=jnp.float32)


def newton_step(iterate, coupled, coupled_full, eye):
    factor = (5.0 * eye - coupled_full) * 0.25
    next_iterate = product(iterate, factor)
    next_coupled = product(product(product(product(coupled, factor), factor), factor), factor)
    return (next_iterate, next_coupled)


def run_iterations(advance, state, count):
    return lax.fori_loop(0, count, advance, state)


def make_folder(grad_rows, left_slab, replica_index, rows_rep):

    def fold_rows(carry, piece, start):
        left_acc = product(grad_rows, piece.T)
        own_cols = lax.dynamic_slice_in_dim(piece, replica_index * rows_rep, rows_rep, 1)
        right_acc = product(own_cols.T, piece)
        half_acc = product(left_slab, piece)
        return (left_acc, right_acc, half_acc)

    return fold_rows


def local(grad_partial, left_stats, right_stats, left_roots, right_roots, newton_counts, owner):
    group = lax.axis_index("refresh")
    owner_index = lax.axis_index(MP)
    replica_index = lax.axis_index(REPLICA)
    owners = lax.axis_size(MP)
    replicas = lax.axis_size(REPLICA)
    rows_part = grad_partial[0, 0]
    rows_mp = rows_part.shape[0]
    order = rows_part.shape[1] // owners
    rows_rep = order // replicas
    owner_row = lax.dynamic_index_in_dim(owner, group, 0, keepdims=False)
    counts_row = lax.dynamic_index_in_dim(newton_counts, group, 0, keepdims=False)
    slots = jnp.arange(owners, dtype=jnp.int32)
    hits = owner_row[:, None] == slots[None, :]
    inverse = jnp.sum(jnp.where(hits, slots[:, None], 0), axis=0)
    count = jnp.sum(jnp.where(owner_row == owner_index, counts_row, 0))
    ordered = jnp.take(rows_part.reshape(rows_mp, owners, order), inverse, axis=1).reshape(
        rows_mp, owners * order
    )
    left_slab = left_roots[0]
    right_slab = right_roots[0]
    zeros = jnp.zeros((rows_rep, order), jnp.float32)
    routed = lax.all_to_all(ordered, MP, split_axis=1, concat_axis=0, tiled=True)
    grad_rows = summed_on_arrival(routed.astype(jnp.float32), REPLICA, 0)
    folder = make_folder(grad_rows, left_slab, replica_index, rows_rep)
    left_term, right_term, half_dir = folder(
        (zeros, zeros, zeros), lax.all_gather(grad_rows, REPLICA, axis=0, tiled=True), jnp.int32(0)
    )
    direction = product(half_dir, lax.all_gather(right_slab, REPLICA, axis=0, tiled=True))
    new_left = decay * left_stats[0] + (1.0 - decay) * left_term
    new_right = decay * right_stats[0] + (1.0 - decay) * right_term
    grad_sq, dir_sq = (
        by_axis(jnp.sum(grad_rows * grad_rows), REPLICA_MP_REFRESH),
        by_axis(jnp.sum(direction * direction), REPLICA_MP_REFRESH),
    )
    scaled = direction * (jnp.sqrt(grad_sq) / jnp.sqrt(dir_sq + graft_eps))
    eye = jnp.eye(order, dtype=jnp.float32)
    left_full, right_full = side_by_side((new_left, new_right), REPLICA, 0, 1)
    parity = replica_index % 2
    chosen = jnp.where(parity == 0, left_full, right_full)
    scale = 2.5 / jnp.sqrt(jnp.sum(chosen * chosen))
    state = (scale**0.25 * eye, scale * chosen)

    def advance_whole(step_index, current):
        return newton_step(current[0], current[1], current[1], eye)

    iterate = run_iterations(advance_whole, state, count)[0]
    partner = replica_index + 1 - 2 * parity
    outgoing = lax.dynamic_slice_in_dim(iterate, partner * rows_rep, rows_rep, 0)
    incoming = swapped(outgoing, REPLICA, 0)
    own_rows = lax.dynamic_slice_in_dim(iterate, replica_index * rows_rep, rows_rep, 0)
    left_root = jnp.where(parity == 0, own_rows, incoming)
    right_root = jnp.where(parity == 0, incoming, own_rows)
    whole_update = gather_directly(scaled, REPLICA, 0)
    returned = lax.all_to_all(whole_update, MP, split_axis=0, concat_axis=1, tiled=True)
    update = jnp.take(returned.reshape(rows_mp, owners, order), owner_row, axis=1).reshape(
        1, rows_mp, owners * order
    )
    return (update, new_left[None], new_right[None], left_root[None], right_root[None])


def solution(mesh):
    finer = Mesh(
        mesh.devices.reshape(8, 2, 8, 2, mesh.shape["refresh"]),
        ("replica_0", "replica_1", "mp_0", "mp_1", "refresh"),
    )
    in_specs = (
        P(REPLICA, "refresh", MP, None),
        P("refresh", REPLICA, MP),
        P("refresh", REPLICA, MP),
        P("refresh", REPLICA, MP),
        P("refresh", REPLICA, MP),
        P(),
        P(),
    )
    out_specs = (
        P("refresh", MP, None),
        P("refresh", REPLICA, MP),
        P("refresh", REPLICA, MP),
        P("refresh", REPLICA, MP),
        P("refresh", REPLICA, MP),
    )
    return jax.shard_map(local, mesh=finer, in_specs=in_specs, out_specs=out_specs, check_vma=False)
```

profile of v0, /device:TPU:1, one launch (start us, length us, event | category | flops | bytes accessed | tf_op | source)
XLA Modules:
  0.0 316.1 jit_solution(1481063598009808224)
XLA Ops:
  10.9 27.2 %all_to_all.33 = bf16[32,16,512]{2,0,1:T(8,128)(2,1)S(1)} all-to-all(bf16[32,16,512]{2,0,1:T(8,128)(2,1)S(1)} %select_bitcast_fusion), channel_id=1, replica_groups=mesh['replica_0'=8,'replica_1'=2,'mp_0'=8,'mp_1'=2,'refresh'=2] {'mp_0',..., dimensions={1} | all-to-all | bytes 1048576 | tf_op jit(solution)/shard_map/all_to_all | solution.py:108
  38.3 41.3 %all_to_all.34 = f32[16,32,512]{2,1,0:T(8,128)S(1)} all-to-all(f32[16,32,512]{2,1,0:T(8,128)S(1)} %convert_bitcast_fusion), channel_id=1, replica_groups=mesh['replica_0'=8,'replica_1'=2,'mp_0'=8,'mp_1'=2,'refresh'=2] {'replic..., dimensions={0} | all-to-all | bytes 2097152 | tf_op jit(solution)/shard_map/all_to_all | solution.py:22
  81.1 31.6 %all-gather.5.cloned.1.call-done = f32[512,512]{1,0:T(8,128)} async-done(((f32[32,512]{1,0:T(8,128)}), f32[512,512]{1,0:T(8,128)}) %all-gather.5.cloned.1.call-update) | async-done | bytes 1048592 | tf_op jit(solution)/shard_map/all_gather | solution.py:112
  112.6 2.1 fusion.43
  114.8 2.3 fusion.42
  119.2 35.6 %all-gather.9.cloned.1.call-done = f32[1,512,512]{2,1,0:T(8,128)} async-done(((f32[1,32,512]{2,1,0:T(8,128)}), f32[1,512,512]{2,1,0:T(8,128)}) %all-gather.9.cloned.1.call-update) | async-done | bytes 1048592 | tf_op jit(solution)/shard_map/all_gather | solution.py:114
  154.8 2.5 multiply_reduce_fusion.1
  157.3 12.4 %all-reduce.1 = (f32[]{:T(128)}, f32[]{:T(128)}) all-reduce(f32[]{:T(128)} %multiply_reduce_fusion.2, f32[]{:T(128)} %get-tuple-element.67), channel_id=1, replica_groups=mesh['replica_0'=8,'replica_1'=2,'mp_0'=8,'mp_1'=2,'refresh'=2] {'replic..., use_global_device_ids=true, to_apply=%region_3.4 | all-reduce | flops 2 | bytes 16 | tf_op jit(solution)/shard_map/psum | solution.py:27
  169.7 6.8 %all-reduce.4 = (f32[]{:T(128)}, f32[]{:T(128)}) all-reduce(f32[]{:T(128)} %get-tuple-element.55, f32[]{:T(128)} %get-tuple-element.56), channel_id=1, replica_groups=mesh['replica_0'=8,'replica_1'=2,'mp_0'=8,'mp_1'=2,'refresh'=2] {'replic..., use_global_device_ids=true, to_apply=%region_4.5 | all-reduce | flops 2 | bytes 16 | tf_op jit(solution)/shard_map/psum | solution.py:27
  176.5 14.4 %all-reduce = (f32[]{:T(128)}, f32[]{:T(128)}) all-reduce(f32[]{:T(128)} %get-tuple-element.61, f32[]{:T(128)} %get-tuple-element.62), channel_id=1, replica_groups=mesh['replica_0'=8,'replica_1'=2,'mp_0'=8,'mp_1'=2,'refresh'=2] {'mp_0'}, use_global_device_ids=true, to_apply=%region_5.6 | all-reduce | flops 2 | bytes 16 | tf_op jit(solution)/shard_map/psum | solution.py:27
  191.0 6.0 %all-reduce.3 = (f32[]{:T(128)}, f32[]{:T(128)}) all-reduce(f32[]{:T(128)} %get-tuple-element.53, f32[]{:T(128)} %get-tuple-element.54), channel_id=1, replica_groups=mesh['replica_0'=8,'replica_1'=2,'mp_0'=8,'mp_1'=2,'refresh'=2] {'mp_1'}, use_global_device_ids=true, to_apply=%region_6.7 | all-reduce | flops 2 | bytes 16 | tf_op jit(solution)/shard_map/psum | solution.py:27
  196.9 4.4 %all-reduce.2 = (f32[]{:T(128)}, f32[]{:T(128)}) all-reduce(f32[]{:T(128)} %get-tuple-element.59, f32[]{:T(128)} %get-tuple-element.60), channel_id=1, replica_groups=mesh['replica_0'=8,'replica_1'=2,'mp_0'=8,'mp_1'=2,'refresh'=2] {'refresh'}, use_global_device_ids=true, to_apply=%region_7.8 | all-reduce | flops 2 | bytes 16 | tf_op jit(solution)/shard_map/psum | solution.py:27
  203.8 11.0 %all-to-all-start.2 = ((f32[16,32,512]{2,1,0:T(8,128)}), f32[16,32,512]{2,1,0:T(8,128)}, u32[]{:S(2)}, u32[]{:S(2)}) async-start(f32[16,32,512]{2,1,0:T(8,128)} %broadcast_in_dim.66), calls=%async_computation.2 | async-start | bytes 2097152 | tf_op jit(solution)/shard_map/all_to_all | solution.py:43
  215.0 28.0 %all-to-all-done.2 = f32[16,32,512]{2,1,0:T(8,128)} async-done(((f32[16,32,512]{2,1,0:T(8,128)}), f32[16,32,512]{2,1,0:T(8,128)}, u32[]{:S(2)}, u32[]{:S(2)}) %all-to-all-start.2) | async-done | bytes 1048608 | tf_op jit(solution)/shard_map/all_to_all | solution.py:43
  242.9 6.7 %all-to-all-start.3 = ((f32[16,32,512]{2,1,0:T(8,128)}), f32[16,32,512]{2,1,0:T(8,128)S(1)}, u32[]{:S(2)}, u32[]{:S(2)}) async-start(f32[16,32,512]{2,1,0:T(8,128)} %all-to-all-done.2), calls=%async_computation.3 | async-start | bytes 2097152 | tf_op jit(solution)/shard_map/all_to_all | solution.py:140
  249.7 2.4 multiply_reduce_fusion
  254.7 48.5 %while.13 = (s32[]{:T(128)}, f32[512,512]{0,1:T(8,128)S(1)}, f32[512,512]{1,0:T(8,128)S(1)}, s32[]{:T(128)}, s32[]{:T(128)}) while((s32[]{:T(128)}, f32[512,512]{0,1:T(8,128)S(1)}, f32[512,512]{1,0:T(8,128)S(1)}, s32[]{:T(128)}, s32[]{:T(128)}) %tuple.29), condition=%wide.region_17.18_spmd.clone, body=%wide.region_16.17_spmd.clone.sunk | while | flops 8058306560 | bytes 18874428 | solution.py:71
  255.7 3.5 %fusion.91 = f32[512,512]{1,0:T(8,128)S(1)} fusion(f32[512,512]{1,0:T(8,128)S(1)} %copy.39), kind=kOutput, calls=%fused_computation.10.clone.1 | convolution fusion | flops 1611661312 | bytes 2097152 | tf_op jit(solution)/shard_map/while/body/dot_general | solution.py:60
  261.1 1.9 fusion.93
  264.9 1.9 fusion.94
  267.6 3.5 %fusion.91 = f32[512,512]{1,0:T(8,128)S(1)} fusion(f32[512,512]{1,0:T(8,128)S(1)} %copy.39), kind=kOutput, calls=%fused_computation.10.clone.1 | convolution fusion | flops 1611661312 | bytes 2097152 | tf_op jit(solution)/shard_map/while/body/dot_general | solution.py:60
  279.6 3.5 %fusion.91 = f32[512,512]{1,0:T(8,128)S(1)} fusion(f32[512,512]{1,0:T(8,128)S(1)} %copy.39), kind=kOutput, calls=%fused_computation.10.clone.1 | convolution fusion | flops 1611661312 | bytes 2097152 | tf_op jit(solution)/shard_map/while/body/dot_general | solution.py:60
  291.5 3.5 %fusion.91 = f32[512,512]{1,0:T(8,128)S(1)} fusion(f32[512,512]{1,0:T(8,128)S(1)} %copy.39), kind=kOutput, calls=%fused_computation.10.clone.1 | convolution fusion | flops 1611661312 | bytes 2097152 | tf_op jit(solution)/shard_map/while/body/dot_general | solution.py:60
  303.7 1.9 collective-permute-start
  (78 shorter events, 42.0 us)
Async XLA Ops:
  7.2 111.3 %copy-start = (f32[1,32,512]{2,1,0:T(8,128)S(1)}, f32[1,32,512]{2,1,0:T(8,128)}, u32[]{:S(2)}) copy-start(f32[1,32,512]{2,1,0:T(8,128)} %param.12) | copy-start | bytes 196612
  7.2 105.5 %all-gather.5.cloned.1.call-start = ((), (), s32[]{:S(2)}) async-start(), calls=%async_computation.4 | async-start | bytes 1114112 | tf_op jit(solution)/shard_map/all_gather | solution.py:112
  38.1 74.5 %copy-start.6 = (f32[1,32,512]{2,1,0:T(8,128)S(1)}, f32[1,32,512]{2,1,0:T(8,128)}, u32[]{:S(2)}) copy-start(f32[1,32,512]{2,1,0:T(8,128)} %param.11) | copy-start | bytes 196612
  38.3 76.5 %copy-start.7 = (f32[1,32,512]{2,1,0:T(8,128)S(1)}, f32[1,32,512]{2,1,0:T(8,128)}, u32[]{:S(2)}) copy-start(f32[1,32,512]{2,1,0:T(8,128)} %param.10) | copy-start | bytes 196612
  80.2 37.6 %copy-start.3 = (f32[32,512]{1,0:T(8,128)S(1)}, f32[32,512]{1,0:T(8,128)}, u32[]{:S(2)}) copy-start(f32[32,512]{1,0:T(8,128)} %reduce_sum.58) | copy-start | bytes 196612
  80.3 74.5 %all-gather.9.cloned.1.call-start = ((), (), s32[]{:S(2)}) async-start(), calls=%async_computation.6 | async-start | bytes 1114112 | tf_op jit(solution)/shard_map/all_gather | solution.py:114
  81.0 168.7 %all-gather.7.cloned.1.call-start = ((), (), s32[]{:S(2)}) async-start(), calls=%async_computation.5 | async-start | bytes 2228224 | tf_op jit(solution)/shard_map/all_gather | solution.py:33
  112.6 5.8 %copy-start.1 = (f32[512,512]{1,0:T(8,128)S(1)}, f32[512,512]{1,0:T(8,128)}, u32[]{:S(2)}) copy-start(f32[512,512]{1,0:T(8,128)} %all-gather.5.cloned.1.call-done) | copy-start | bytes 3145732
  114.8 87.9 %copy-start.4 = (f32[32,512]{1,0:T(8,128)}, f32[32,512]{1,0:T(8,128)S(1)}, u32[]{:S(2)}) copy-start(f32[32,512]{1,0:T(8,128)S(1)} %fusion.43) | copy-start | bytes 196612
  117.1 86.7 %copy-start.5 = (f32[32,512]{1,0:T(8,128)}, f32[32,512]{1,0:T(8,128)S(1)}, u32[]{:S(2)}) copy-start(f32[32,512]{1,0:T(8,128)S(1)} %fusion.42) | copy-start | bytes 196612
  119.2 95.7 %copy-start.8 = (s32[2,16]{1,0:T(2,128)S(1)}, s32[2,16]{1,0:T(2,128)}, u32[]{:S(2)}) copy-start(s32[2,16]{1,0:T(2,128)} %param.15) | copy-start | bytes 388
  203.8 39.1 %all-to-all-start.2 = ((f32[16,32,512]{2,1,0:T(8,128)}), f32[16,32,512]{2,1,0:T(8,128)}, u32[]{:S(2)}, u32[]{:S(2)}) async-start(f32[16,32,512]{2,1,0:T(8,128)} %broadcast_in_dim.66), calls=%async_computation.2 | async-start | bytes 2097152 | tf_op jit(solution)/shard_map/all_to_all | solution.py:43
  242.9 62.7 %all-to-all-start.3 = ((f32[16,32,512]{2,1,0:T(8,128)}), f32[16,32,512]{2,1,0:T(8,128)S(1)}, u32[]{:S(2)}, u32[]{:S(2)}) async-start(f32[16,32,512]{2,1,0:T(8,128)} %all-to-all-done.2), calls=%async_computation.3 | async-start | bytes 2097152 | tf_op jit(solution)/shard_map/all_to_all | solution.py:140
  303.6 2.6 copy-start.2
  303.7 4.5 %collective-permute-start = (f32[32,512]{1,0:T(8,128)S(1)}, f32[32,512]{1,0:T(8,128)S(1)}, u32[]{:S(2)}, u32[]{:S(2)}) collective-permute-start(f32[32,512]{1,0:T(8,128)S(1)} %constant_dynamic-slice_fusion), channel_id=1, source_target_pairs={{0,32},{32,0},{64,96},{96,64},{128,160},{160,128},{192,224},{224,1... | collective-permute-start | bytes 196616 | tf_op jit(solution)/shard_map/ppermute | solution.py:38
Sparse Core Ops, SparseCore 0:
  80.4 32.2 all-gather.4
  114.8 39.9 all-gather.8
  156.9 40.9 all-gather.6
where the time goes:
time: 317 us; the launch traced here: 316 us
  blocking collectives  112 us (35%)
  waiting for transfers between devices  95.9 us (30%)
  matrix products  52.1 us (16%)
  starting transfers between devices  19.8 us (6%)
  between operations  16.2 us (5%)
  other arithmetic  10.6 us (3%)
  local copies, waits for them, and re-layouts  5.64 us (2%)
  loops' own time  3.56 us (1%)
    dot_general x24, matrix products, product(): jnp.dot(left, right, precision=lax.Precision.HIGHEST, preferred_element_t...  52.1 us
    psum x5, blocking collectives, by_axis(): return functools.reduce(lax.psum, axes, shard)  44 us
    all_to_all x1, blocking collectives, summed_on_arrival(): lax.all_to_all(tiles, axis, split_axis=0, concat_axis=0, tiled=True)  41.3 us
    all_gather x1, waiting for transfers between devices, local(): lax.all_gather(right_slab, REPLICA, axis=0, tiled=True)  35.6 us
    all_gather x1, waiting for transfers between devices, local(): lax.all_gather(grad_rows, REPLICA, axis=0, tiled=True)  31.6 us
    all_to_all x1, waiting for transfers between devices, sent_to_all(): lax.all_to_all(jnp.broadcast_to(shard[None], (count, *shard.shape)), axis...  28 us
    all_to_all x1, blocking collectives, local(): lax.all_to_all(ordered, MP, split_axis=1, concat_axis=0, tiled=True)  27.2 us
    all_to_all x1, starting transfers between devices, sent_to_all(): lax.all_to_all(jnp.broadcast_to(shard[None], (count, *shard.shape)), axis...  11 us
  transfers between devices with their start and end apart: 6, of which 3 were waited for; matrix products, arithmetic and copies ran while one was open for 20% of the time, Pallas kernels for 0%

commit v1 on v0

--- a/solution.py
+++ b/solution.py
@@ -10,6 +10,11 @@
 REPLICA_MP_REFRESH = ("replica_0", "replica_1", "mp_0", "mp_1", "refresh")
 decay = 0.9
 graft_eps = 1e-06
+
+
+def exchange_gather(array, axis, dim):
+    repeated = jnp.stack([array] * lax.axis_size(axis))
+    return jnp.concatenate(lax.all_to_all(repeated, axis, 0, 0), axis=dim)
 
 
 def split_up(shard, dim, count):
@@ -109,7 +114,7 @@
     grad_rows = summed_on_arrival(routed.astype(jnp.float32), REPLICA, 0)
     folder = make_folder(grad_rows, left_slab, replica_index, rows_rep)
     left_term, right_term, half_dir = folder(
-        (zeros, zeros, zeros), lax.all_gather(grad_rows, REPLICA, axis=0, tiled=True), jnp.int32(0)
+        (zeros, zeros, zeros), exchange_gather(grad_rows, REPLICA, 0), jnp.int32(0)
     )
     direction = product(half_dir, lax.all_gather(right_slab, REPLICA, axis=0, tiled=True))
     new_left = decay * left_stats[0] + (1.0 - decay) * left_term

time: 317 us -> 287 us (0.905)
  waiting for transfers between devices: 95.9 us -> 66.2 us
    all_gather x1 -> x0, waiting for transfers between devices: 31.6 us -> none  [local(): lax.all_gather(grad_rows, REPLICA, axis=0, tiled=True)]
    all_to_all x0 -> x1, waiting for transfers between devices: none -> 28.6 us  [exchange_gather(): return jnp.concatenate(lax.all_to_all(repeated, axis, 0, 0), axis=dim)]
    all_gather x1, waiting for transfers between devices: 35.6 us -> 9 us  [local(): lax.all_gather(right_slab, REPLICA, axis=0, tiled=True)]
    all_to_all x0 -> x1, starting transfers between devices: none -> 3.55 us  [exchange_gather(): return jnp.concatenate(lax.all_to_all(repeated, axis, 0, 0), axis=dim)]
  transfers between devices with their start and end apart: 6 -> 6, of which waited for: 3 -> 3; matrix products, arithmetic and copies ran while one was open for 20% -> 21% of each run, Pallas kernels for 0% -> 0%
where the time goes in v1:
time: 287 us; the launch traced here: 286 us
  blocking collectives  112 us (39%)
  waiting for transfers between devices  66.2 us (23%)
  matrix products  49.5 us (17%)
  starting transfers between devices  21.2 us (7%)
  between operations  16.4 us (6%)
  other arithmetic  9.95 us (3%)
  local copies, waits for them, and re-layouts  6.73 us (2%)
  loops' own time  3.69 us (1%)
    dot_general x24, matrix products, product(): jnp.dot(left, right, precision=lax.Precision.HIGHEST, preferred_element_t...  49.5 us
    psum x5, blocking collectives, by_axis(): return functools.reduce(lax.psum, axes, shard)  44.1 us
    all_to_all x1, blocking collectives, summed_on_arrival(): lax.all_to_all(tiles, axis, split_axis=0, concat_axis=0, tiled=True)  41.1 us
    all_to_all x1, waiting for transfers between devices, exchange_gather(): return jnp.concatenate(lax.all_to_all(repeated, axis, 0, 0), axis=dim)  28.6 us
    all_to_all x1, waiting for transfers between devices, sent_to_all(): lax.all_to_all(jnp.broadcast_to(shard[None], (count, *shard.shape)), axis...  28 us
    all_to_all x1, blocking collectives, local(): lax.all_to_all(ordered, MP, split_axis=1, concat_axis=0, tiled=True)  27.2 us
    all_to_all x1, starting transfers between devices, sent_to_all(): lax.all_to_all(jnp.broadcast_to(shard[None], (count, *shard.shape)), axis...  9.66 us
    all_gather x1, waiting for transfers between devices, local(): lax.all_gather(right_slab, REPLICA, axis=0, tiled=True)  9 us
  transfers between devices with their start and end apart: 6, of which 3 were waited for; matrix products, arithmetic and copies ran while one was open for 21% of the time, Pallas kernels for 0%

profile of v1, /device:TPU:1, one launch (start us, length us, event | category | flops | bytes accessed | tf_op | source)
XLA Modules:
  0.0 286.2 jit_solution(1271501867535731050)
XLA Ops:
  10.9 27.2 %all_to_all.38 = bf16[32,16,512]{2,0,1:T(8,128)(2,1)S(1)} all-to-all(bf16[32,16,512]{2,0,1:T(8,128)(2,1)S(1)} %select_bitcast_fusion), channel_id=1, replica_groups=mesh['replica_0'=8,'replica_1'=2,'mp_0'=8,'mp_1'=2,'refresh'=2] {'mp_0',..., dimensions={1} | all-to-all | bytes 1048576 | tf_op jit(solution)/shard_map/all_to_all | solution.py:113
  38.2 41.1 %all_to_all.39 = f32[16,32,512]{2,1,0:T(8,128)S(1)} all-to-all(f32[16,32,512]{2,1,0:T(8,128)S(1)} %convert_bitcast_fusion), channel_id=1, replica_groups=mesh['replica_0'=8,'replica_1'=2,'mp_0'=8,'mp_1'=2,'refresh'=2] {'replic..., dimensions={0} | all-to-all | bytes 2097152 | tf_op jit(solution)/shard_map/all_to_all | solution.py:27
  80.5 3.6 %all-to-all-start.2 = ((f32[16,32,512]{2,1,0:T(8,128)}), f32[16,32,512]{2,1,0:T(8,128)S(1)}, u32[]{:S(2)}, u32[]{:S(2)}) async-start(f32[16,32,512]{2,1,0:T(8,128)} %stack.2), calls=%async_computation.2 | async-start | bytes 2097152 | tf_op jit(solution)/shard_map/all_to_all | solution.py:17
  84.9 28.6 %all-to-all-done.2 = f32[16,32,512]{2,1,0:T(8,128)S(1)} async-done(((f32[16,32,512]{2,1,0:T(8,128)}), f32[16,32,512]{2,1,0:T(8,128)S(1)}, u32[]{:S(2)}, u32[]{:S(2)}) %all-to-all-start.2) | async-done | bytes 1048608 | tf_op jit(solution)/shard_map/all_to_all | solution.py:17
  117.4 9.0 %all-gather.6.cloned.1.call-done = f32[1,512,512]{2,1,0:T(8,128)} async-done(((f32[1,32,512]{2,1,0:T(8,128)}), f32[1,512,512]{2,1,0:T(8,128)}) %all-gather.6.cloned.1.call-update) | async-done | bytes 1048592 | tf_op jit(solution)/shard_map/all_gather | solution.py:119
  126.4 2.5 multiply_reduce_fusion.1
  128.9 13.5 %all-reduce.1 = (f32[]{:T(128)}, f32[]{:T(128)}) all-reduce(f32[]{:T(128)} %multiply_reduce_fusion.2, f32[]{:T(128)} %get-tuple-element.67), channel_id=1, replica_groups=mesh['replica_0'=8,'replica_1'=2,'mp_0'=8,'mp_1'=2,'refresh'=2] {'replic..., use_global_device_ids=true, to_apply=%region_3.4 | all-reduce | flops 2 | bytes 16 | tf_op jit(solution)/shard_map/psum | solution.py:32
  142.4 6.8 %all-reduce.4 = (f32[]{:T(128)}, f32[]{:T(128)}) all-reduce(f32[]{:T(128)} %get-tuple-element.55, f32[]{:T(128)} %get-tuple-element.56), channel_id=1, replica_groups=mesh['replica_0'=8,'replica_1'=2,'mp_0'=8,'mp_1'=2,'refresh'=2] {'replic..., use_global_device_ids=true, to_apply=%region_4.5 | all-reduce | flops 2 | bytes 16 | tf_op jit(solution)/shard_map/psum | solution.py:32
  149.2 13.5 %all-reduce = (f32[]{:T(128)}, f32[]{:T(128)}) all-reduce(f32[]{:T(128)} %get-tuple-element.61, f32[]{:T(128)} %get-tuple-element.62), channel_id=1, replica_groups=mesh['replica_0'=8,'replica_1'=2,'mp_0'=8,'mp_1'=2,'refresh'=2] {'mp_0'}, use_global_device_ids=true, to_apply=%region_5.6 | all-reduce | flops 2 | bytes 16 | tf_op jit(solution)/shard_map/psum | solution.py:32
  162.7 5.9 %all-reduce.3 = (f32[]{:T(128)}, f32[]{:T(128)}) all-reduce(f32[]{:T(128)} %get-tuple-element.53, f32[]{:T(128)} %get-tuple-element.54), channel_id=1, replica_groups=mesh['replica_0'=8,'replica_1'=2,'mp_0'=8,'mp_1'=2,'refresh'=2] {'mp_1'}, use_global_device_ids=true, to_apply=%region_6.7 | all-reduce | flops 2 | bytes 16 | tf_op jit(solution)/shard_map/psum | solution.py:32
  168.6 4.4 %all-reduce.2 = (f32[]{:T(128)}, f32[]{:T(128)}) all-reduce(f32[]{:T(128)} %get-tuple-element.59, f32[]{:T(128)} %get-tuple-element.60), channel_id=1, replica_groups=mesh['replica_0'=8,'replica_1'=2,'mp_0'=8,'mp_1'=2,'refresh'=2] {'refresh'}, use_global_device_ids=true, to_apply=%region_7.8 | all-reduce | flops 2 | bytes 16 | tf_op jit(solution)/shard_map/psum | solution.py:32
  175.5 9.7 %all-to-all-start.3 = ((f32[16,32,512]{2,1,0:T(8,128)}), f32[16,32,512]{2,1,0:T(8,128)}, u32[]{:S(2)}, u32[]{:S(2)}) async-start(f32[16,32,512]{2,1,0:T(8,128)} %broadcast_in_dim.66), calls=%async_computation.3 | async-start | bytes 2097152 | tf_op jit(solution)/shard_map/all_to_all | solution.py:48
  185.3 28.0 %all-to-all-done.3 = f32[16,32,512]{2,1,0:T(8,128)} async-done(((f32[16,32,512]{2,1,0:T(8,128)}), f32[16,32,512]{2,1,0:T(8,128)}, u32[]{:S(2)}, u32[]{:S(2)}) %all-to-all-start.3) | async-done | bytes 1048608 | tf_op jit(solution)/shard_map/all_to_all | solution.py:48
  213.2 6.0 %all-to-all-start.4 = ((f32[16,32,512]{2,1,0:T(8,128)}), f32[16,32,512]{2,1,0:T(8,128)S(1)}, u32[]{:S(2)}, u32[]{:S(2)}) async-start(f32[16,32,512]{2,1,0:T(8,128)} %all-to-all-done.3), calls=%async_computation.4 | async-start | bytes 2097152 | tf_op jit(solution)/shard_map/all_to_all | solution.py:145
  219.3 2.4 multiply_reduce_fusion
  224.3 48.7 %while.13 = (s32[]{:T(128)}, f32[512,512]{0,1:T(8,128)S(1)}, f32[512,512]{1,0:T(8,128)S(1)}, s32[]{:T(128)}, s32[]{:T(128)}) while((s32[]{:T(128)}, f32[512,512]{0,1:T(8,128)S(1)}, f32[512,512]{1,0:T(8,128)S(1)}, s32[]{:T(128)}, s32[]{:T(128)}) %tuple.29), condition=%wide.region_17.18_spmd.clone, body=%wide.region_16.17_spmd.clone.sunk | while | flops 8058306560 | bytes 18874428 | solution.py:76
  225.3 3.5 %fusion.91 = f32[512,512]{1,0:T(8,128)S(1)} fusion(f32[512,512]{1,0:T(8,128)S(1)} %copy.39), kind=kOutput, calls=%fused_computation.10.clone.1 | convolution fusion | flops 1611661312 | bytes 2097152 | tf_op jit(solution)/shard_map/while/body/dot_general | solution.py:65
  230.7 1.9 fusion.93
  234.6 1.9 fusion.94
  237.3 3.5 %fusion.91 = f32[512,512]{1,0:T(8,128)S(1)} fusion(f32[512,512]{1,0:T(8,128)S(1)} %copy.39), kind=kOutput, calls=%fused_computation.10.clone.1 | convolution fusion | flops 1611661312 | bytes 2097152 | tf_op jit(solution)/shard_map/while/body/dot_general | solution.py:65
  242.7 1.9 fusion.93
  249.2 3.5 %fusion.91 = f32[512,512]{1,0:T(8,128)S(1)} fusion(f32[512,512]{1,0:T(8,128)S(1)} %copy.39), kind=kOutput, calls=%fused_computation.10.clone.1 | convolution fusion | flops 1611661312 | bytes 2097152 | tf_op jit(solution)/shard_map/while/body/dot_general | solution.py:65
  261.2 3.5 %fusion.91 = f32[512,512]{1,0:T(8,128)S(1)} fusion(f32[512,512]{1,0:T(8,128)S(1)} %copy.39), kind=kOutput, calls=%fused_computation.10.clone.1 | convolution fusion | flops 1611661312 | bytes 2097152 | tf_op jit(solution)/shard_map/while/body/dot_general | solution.py:65
  273.4 1.9 collective-permute-start
  (74 shorter events, 42.3 us)
Async XLA Ops:
  7.2 109.4 %copy-start = (f32[1,32,512]{2,1,0:T(8,128)S(1)}, f32[1,32,512]{2,1,0:T(8,128)}, u32[]{:S(2)}) copy-start(f32[1,32,512]{2,1,0:T(8,128)} %param.12) | copy-start | bytes 196612
  79.4 34.1 %copy-start.4 = (f32[1,32,512]{2,1,0:T(8,128)S(1)}, f32[1,32,512]{2,1,0:T(8,128)}, u32[]{:S(2)}) copy-start(f32[1,32,512]{2,1,0:T(8,128)} %param.11) | copy-start | bytes 196612
  79.4 34.8 %copy-start.5 = (f32[1,32,512]{2,1,0:T(8,128)S(1)}, f32[1,32,512]{2,1,0:T(8,128)}, u32[]{:S(2)}) copy-start(f32[1,32,512]{2,1,0:T(8,128)} %param.10) | copy-start | bytes 196612
  80.5 32.9 %all-to-all-start.2 = ((f32[16,32,512]{2,1,0:T(8,128)}), f32[16,32,512]{2,1,0:T(8,128)S(1)}, u32[]{:S(2)}, u32[]{:S(2)}) async-start(f32[16,32,512]{2,1,0:T(8,128)} %stack.2), calls=%async_computation.2 | async-start | bytes 2097152 | tf_op jit(solution)/shard_map/all_to_all | solution.py:17
  84.1 42.2 %all-gather.6.cloned.1.call-start = ((), (), s32[]{:S(2)}) async-start(), calls=%async_computation.6 | async-start | bytes 1114112 | tf_op jit(solution)/shard_map/all_gather | solution.py:119
  84.8 134.4 %all-gather.4.cloned.1.call-start = ((), (), s32[]{:S(2)}) async-start(), calls=%async_computation.5 | async-start | bytes 2228224 | tf_op jit(solution)/shard_map/all_gather | solution.py:38
  114.2 60.1 %copy-start.2 = (f32[32,512]{1,0:T(8,128)}, f32[32,512]{1,0:T(8,128)S(1)}, u32[]{:S(2)}) copy-start(f32[32,512]{1,0:T(8,128)S(1)} %fusion.43) | copy-start | bytes 196612
  115.3 60.2 %copy-start.3 = (f32[32,512]{1,0:T(8,128)}, f32[32,512]{1,0:T(8,128)S(1)}, u32[]{:S(2)}) copy-start(f32[32,512]{1,0:T(8,128)S(1)} %fusion.42) | copy-start | bytes 196612
  117.3 67.9 %copy-start.6 = (s32[2,16]{1,0:T(2,128)S(1)}, s32[2,16]{1,0:T(2,128)}, u32[]{:S(2)}) copy-start(s32[2,16]{1,0:T(2,128)} %param.15) | copy-start | bytes 388
  175.5 37.8 %all-to-all-start.3 = ((f32[16,32,512]{2,1,0:T(8,128)}), f32[16,32,512]{2,1,0:T(8,128)}, u32[]{:S(2)}, u32[]{:S(2)}) async-start(f32[16,32,512]{2,1,0:T(8,128)} %broadcast_in_dim.66), calls=%async_computation.3 | async-start | bytes 2097152 | tf_op jit(solution)/shard_map/all_to_all | solution.py:48
  213.2 62.1 %all-to-all-start.4 = ((f32[16,32,512]{2,1,0:T(8,128)}), f32[16,32,512]{2,1,0:T(8,128)S(1)}, u32[]{:S(2)}, u32[]{:S(2)}) async-start(f32[16,32,512]{2,1,0:T(8,128)} %all-to-all-done.3), calls=%async_computation.4 | async-start | bytes 2097152 | tf_op jit(solution)/shard_map/all_to_all | solution.py:145
  273.3 2.6 copy-start.1
  273.4 4.5 %collective-permute-start = (f32[32,512]{1,0:T(8,128)S(1)}, f32[32,512]{1,0:T(8,128)S(1)}, u32[]{:S(2)}, u32[]{:S(2)}) collective-permute-start(f32[32,512]{1,0:T(8,128)S(1)} %constant_dynamic-slice_fusion), channel_id=1, source_target_pairs={{0,32},{32,0},{64,96},{96,64},{128,160},{160,128},{192,224},{224,1... | collective-permute-start | bytes 196616 | tf_op jit(solution)/shard_map/ppermute | solution.py:43
Sparse Core Ops, SparseCore 0:
  87.0 39.2 all-gather.5
  128.5 38.9 all-gather.3
